TPU v7x, 256 devices: a whole 4x4x8 slice. The times are simulated.
256 devices in a mesh: seg: 64 (over z, x, core), bin: 4 (over y).
Axes of the slice: x: 4, y: 4, z: 8, core: 2. Of those that a mesh axis runs over, the one named last changes fastest.
Arguments:
- magnet_real: bfloat16 [512, 8, 32768], P('seg', None, 'bin'), may hold values from -8 to 8
- magnet_imag: bfloat16 [512, 8, 32768], P('seg', None, 'bin'), may hold values from -8 to 8
- detector_real: bfloat16 [512, 2, 32768], P('seg', None, 'bin'), may hold values from -8 to 8
- detector_imag: bfloat16 [512, 2, 32768], P('seg', None, 'bin'), may hold values from -8 to 8
- valid: int32 [512], P('seg'), may hold values 0 or 1
- intersection: float32 [32768], P('bin'), may hold values from 0.1 to 1
Outputs:
- cleaned_real: float32 [512, 32768], P('seg', 'bin')
- cleaned_imag: float32 [512, 32768], P('seg', 'bin')
- estimate: float32 [512], P('seg')
Inputs may be any that keep to these rules, and one draw needn't show every extreme that they name: `valid`: 1 keeps a segment in the spectral sums, 0 vetoes it.
All inputs are finite; a program needn't handle non-finite values. No bound on the sum of `valid` on one device may be relied on, other than what follows from the above.
Results may differ from a plain program's by a relative error of at most 0.0005.
Values sent between devices are 32-bit elements; how exact they have to be, the bound alone decides.
A program may use at most 64 MiB of HBM per device.

v0:
```python
import jax
import jax.numpy as jnp
from jax import lax
from jax.sharding import Mesh
from jax.sharding import PartitionSpec as P

SEG = ("seg_0", "seg_1", "seg_2")


def summed_rows(shard, axes, dim):
    for axis in axes:
        shard = lax.psum_scatter(shard, axis, scatter_dimension=dim, tiled=True)
    return shard


def sent_together(arrays, axis, dim, along):
    both = jnp.concatenate(arrays, axis=along)
    whole, at, gathered = (lax.all_gather(both, axis, axis=dim, tiled=True), 0, [])
    for a in arrays:
        gathered.append(lax.slice_in_dim(whole, at, at + a.shape[along], axis=along))
        at += a.shape[along]
    return tuple(gathered)


def wiener_solve(s_real, s_imag, p_real, p_imag):
    channels = s_real.shape[0]
    matrix_size = 2 * channels

    def matrix_entry(i, j):
        if i < channels and j < channels:
            value = s_real[i, j]
        elif j < channels:
            value = s_imag[i - channels, j]
        else:
            value = s_real[i - channels, j - channels]
        if i == j:
            value = value + 1.0
        return value

    def right_entry(i):
        if i < channels:
            return p_real[i]
        return p_imag[i - channels]

    factor = [[None] * matrix_size for i in range(matrix_size)]
    for j in range(matrix_size):
        running = matrix_entry(j, j)
        for k in range(j):
            running = running - factor[j][k] * factor[j][k]
        factor[j][j] = jnp.sqrt(running)
        inverse = 1.0 / factor[j][j]
        for i in range(j + 1, matrix_size):
            running = matrix_entry(i, j)
            for k in range(j):
                running = running - factor[i][k] * factor[j][k]
            factor[i][j] = running * inverse
    forward = []
    for i in range(matrix_size):
        running = right_entry(i)
        for k in range(i):
            running = running - factor[i][k] * forward[k]
        forward.append(running / factor[i][i])
    backward = [None] * matrix_size
    for i in reversed(range(matrix_size)):
        running = forward[i]
        for k in range(i + 1, matrix_size):
            running = running - factor[k][i] * backward[k]
        backward[i] = running / factor[i][i]
    return (jnp.stack(backward[:channels]), jnp.stack(backward[channels:]))


def cross_spectra(magnet_real, magnet_imag, detector_real, detector_imag, valid):
    keep = valid.astype(jnp.float32)[:, None]
    channels = magnet_real.shape[1]
    s_real_rows = []
    s_imag_rows = []
    p_real_rows = []
    p_imag_rows = []
    for chan in range(channels):
        left_real = (magnet_real[:, chan].astype(jnp.float32) * keep)[:, None, :]
        left_imag = (magnet_imag[:, chan].astype(jnp.float32) * keep)[:, None, :]
        s_real_rows.append(
            jnp.sum(
                left_real * magnet_real.astype(jnp.float32)
                + left_imag * magnet_imag.astype(jnp.float32),
                axis=0,
            )
        )
        s_imag_rows.append(
            jnp.sum(
                left_imag * magnet_real.astype(jnp.float32)
                - left_real * magnet_imag.astype(jnp.float32),
                axis=0,
            )
        )
        p_real_rows.append(
            jnp.sum(
                left_real * detector_real.astype(jnp.float32)
                + left_imag * detector_imag.astype(jnp.float32),
                axis=0,
            )
        )
        p_imag_rows.append(
            jnp.sum(
                left_imag * detector_real.astype(jnp.float32)
                - left_real * detector_imag.astype(jnp.float32),
                axis=0,
            )
        )
    return (
        jnp.stack(s_real_rows),
        jnp.stack(s_imag_rows),
        jnp.stack(p_real_rows),
        jnp.stack(p_imag_rows),
    )


def pack_spectra(s_real, s_imag, p_real, p_imag):
    bin_count = s_real.shape[2]
    pieces = [s_real.reshape(-1, bin_count), s_imag.reshape(-1, bin_count)]
    pieces = pieces + [p_real.reshape(-1, bin_count), p_imag.reshape(-1, bin_count)]
    return jnp.concatenate(pieces, axis=0)


def unpack_spectra(packed, channels, detectors):
    bin_count = packed.shape[1]
    square_count = channels * channels
    s_real = packed[:square_count].reshape(channels, channels, bin_count)
    s_imag = packed[square_count : 2 * square_count].reshape(channels, channels, bin_count)
    cross_rows = packed[2 * square_count :]
    cross_count = channels * detectors
    p_real = cross_rows[:cross_count].reshape(channels, detectors, bin_count)
    p_imag = cross_rows[cross_count:].reshape(channels, detectors, bin_count)
    return (s_real, s_imag, p_real, p_imag)


def on_device(magnet_real, magnet_imag, detector_real, detector_imag, valid, intersection):
    s_real, s_imag, p_real, p_imag = cross_spectra(
        magnet_real, magnet_imag, detector_real, detector_imag, valid
    )
    channels = s_real.shape[0]
    detectors = p_real.shape[1]
    packed = pack_spectra(s_real, s_imag, p_real, p_imag)
    shared_spectra = summed_rows(packed, SEG, 1)
    share_real, share_imag = wiener_solve(*unpack_spectra(shared_spectra, channels, detectors))
    filt_real, filt_imag = sent_together((share_real, share_imag), SEG, 2, 0)
    clean_real = detector_real.astype(jnp.float32)
    clean_imag = detector_imag.astype(jnp.float32)
    for chan in range(channels):
        field_real = magnet_real[:, chan].astype(jnp.float32)[:, None, :]
        field_imag = magnet_imag[:, chan].astype(jnp.float32)[:, None, :]
        weight_real = filt_real[chan][None, :, :]
        weight_imag = filt_imag[chan][None, :, :]
        clean_real = clean_real - weight_real * field_real - weight_imag * field_imag
        clean_imag = clean_imag - weight_real * field_imag + weight_imag * field_real
    cleaned_real = clean_real[:, 0] * clean_real[:, 1] + clean_imag[:, 0] * clean_imag[:, 1]
    cleaned_imag = clean_imag[:, 0] * clean_real[:, 1] - clean_real[:, 0] * clean_imag[:, 1]
    numerator = jnp.sum(cleaned_real * intersection[None, :], axis=1)
    weight_square = jnp.sum(intersection * intersection)
    summed, norm_square = lax.psum((numerator, weight_square), "bin")
    estimate = summed / jnp.sqrt(norm_square)
    return (cleaned_real, cleaned_imag, estimate)


def solution(mesh):
    torus = Mesh(
        mesh.devices.reshape(8, 4, 2, mesh.shape["bin"]), ("seg_0", "seg_1", "seg_2", "bin")
    )
    in_specs = (
        P(SEG, None, "bin"),
        P(SEG, None, "bin"),
        P(SEG, None, "bin"),
        P(SEG, None, "bin"),
        P(SEG),
        P("bin"),
    )
    out_specs = (P(SEG, "bin"), P(SEG, "bin"), P(SEG))
    return jax.shard_map(
        on_device, mesh=torus, in_specs=in_specs, out_specs=out_specs, check_vma=False
    )
```

profile of v0, /device:TPU:1, one launch (start us, length us, event | category | flops | bytes accessed | tf_op | source)
XLA Modules:
  0.0 241.9 jit_solution(8950154593771467322)
XLA Ops:
  7.2 0.0 reduce-scatter.4.cloned.1.call-start
  7.2 6.6 %fusion.416 = (bf16[8,1,8192]{2,1,0:T(2,128)(2,1)S(1)}, bf16[8,1,8192]{2,1,0:T(2,128)(2,1)S(1)}, bf16[8,1,8192]{2,1,0:T(2,128)(2,1)S(1)}, bf16[8,1,8192]{2,1,0:T...) fusion(bf16[8,8,8192]{2,1,0:T(8,128)(2,1)} %param.7), kind=kLoop, calls=%fused_computation.776 | loop fusion | bytes 2097152 | tf_op jit(solution)/shard_map/slice | solution.py:81
  13.8 0.0 copy-done.36
  13.8 0.0 copy-start.7
  13.8 0.0 copy-start.8
  13.9 2.2 fusion.417
  16.1 0.0 copy-start.5
  16.1 0.0 copy-start.6
  16.1 0.0 copy-start
  16.1 3.4 %fusion.95 = (f32[8,8192]{1,0:T(8,128)S(1)}, f32[8,8192]{1,0:T(8,128)S(1)}, f32[8,8192]{1,0:T(8,128)S(1)}, f32[8,8192]{1,0:T(8,128)S(1)}, f32[8,8192]{1,0:T(8,12...) fusion(f32[8]{0:T(128)S(1)} %convert_element_type.76, ...), kind=kLoop, calls=%fused_computation.194 | loop fusion | flops 2097152 | bytes 6291488 | tf_op jit(solution)/shard_map/mul | solution.py:85
  19.6 0.0 copy-start.17
  19.6 0.0 copy-start.19
  19.6 7.1 %fusion.15 = (f32[8,8192]{1,0:T(8,128)}, f32[8,8192]{1,0:T(8,128)}, f32[8,8192]{1,0:T(8,128)}, f32[8,8192]{1,0:T(8,128)}, f32[8,8192]{1,0:T(8,128)}, /*index=5*/...) fusion(bf16[8,8,8192]{2,1,0:T(8,128)(2,1)S(1)} %copy-done.1, ...), kind=kLoop, calls=%fused_computation.82 | loop fusion | flops 33554432 | bytes 10485760 | tf_op jit(solution)/shard_map/reduce_sum | solution.py:83
  26.7 3.7 %fusion.47 = (f32[2,8192]{1,0:T(2,128)S(1)}, f32[2,8192]{1,0:T(2,128)S(1)}, f32[2,8192]{1,0:T(2,128)S(1)}, f32[2,8192]{1,0:T(2,128)S(1)}, f32[2,8192]{1,0:T(2,12...) fusion(f32[8,8192]{1,0:T(8,128)S(1)} %get-tuple-element.282, ...), kind=kLoop, calls=%fused_computation.114 | loop fusion | flops 8388608 | bytes 5767168 | tf_op jit(solution)/shard_map/reduce_sum | solution.py:97
  30.7 0.8 copy-done.33
  31.5 0.4 reshape.28781
  31.8 1.4 reshape.28780
  33.3 1.1 bitcast_dynamic-update-slice_fusion.7
  34.4 1.0 bitcast_dynamic-update-slice_fusion.15
  35.4 1.0 bitcast_dynamic-update-slice_fusion.6
  36.4 1.0 bitcast_dynamic-update-slice_fusion.5
  37.5 0.0 copy-start.31
  37.6 0.0 copy-start.32
  37.8 0.6 copy-done.22
  38.4 0.1 copy-done.21
  38.5 0.1 copy-done.31
  38.6 0.1 copy-done.32
  38.7 2.5 %pad_maximum_fusion = f32[160,8192]{1,0:T(8,128)} fusion(f32[16,8192]{1,0:T(8,128)S(1)} %reshape.28781, f32[16,8192]{1,0:T(8,128)S(1)} %reshape.28780, f32[64,8192]{1,0:T(8,128)S(1)} %bitcast.1228, f32[64,8192]{1,0:T(8,128)S(1)} %bitcast.1227), kind=kLoop, calls=%fused_computation.32 | loop fusion | flops 3932160 | bytes 10485760 | tf_op jit(solution)/shard_map/concatenate | solution.py:122
  41.2 0.0 reduce-scatter.4.cloned.1.call-update
  41.3 0.0 reduce-scatter.6.cloned.1.call-start
  41.3 0.3 convert_bitcast_fusion
  41.6 1.3 convert_bitcast_fusion.1
  43.0 0.3 convert_bitcast_fusion.4
  43.3 0.3 convert_bitcast_fusion.5
  43.6 66.7 %reduce-scatter.4.cloned.1.call-done = f32[160,1024]{1,0:T(8,128)} async-done(((f32[160,8192]{1,0:T(8,128)}), f32[160,1024]{1,0:T(8,128)}) %reduce-scatter.4.cloned.1.call-update) | async-done | bytes 655376 | tf_op jit(solution)/shard_map/reduce_scatter | solution.py:12
  110.4 0.0 reduce-scatter.6.cloned.1.call-update
  110.4 0.0 copy-start.34
  110.4 0.0 reduce-scatter.8.cloned.1.call-start
  110.5 2.0 convert_bitcast_fusion.8
  112.5 21.9 %reduce-scatter.6.cloned.1.call-done = f32[160,256]{1,0:T(8,128)} async-done(((f32[160,1024]{1,0:T(8,128)}), f32[160,256]{1,0:T(8,128)}) %reduce-scatter.6.cloned.1.call-update) | async-done | bytes 163856 | tf_op jit(solution)/shard_map/reduce_scatter | solution.py:12
  134.4 0.0 reduce-scatter.8.cloned.1.call-update
  134.4 0.0 all-gather.2.cloned.1.call-start
  134.5 2.1 convert_bitcast_fusion.9
  136.6 15.5 %reduce-scatter.8.cloned.1.call-done = f32[160,128]{1,0:T(8,128)} async-done(((f32[160,256]{1,0:T(8,128)}), f32[160,128]{1,0:T(8,128)}) %reduce-scatter.8.cloned.1.call-update) | async-done | bytes 81936 | tf_op jit(solution)/shard_map/reduce_scatter | solution.py:12
  152.1 0.8 slice_bitcast_fusion.16
  152.9 0.3 sqrt_multiply_fusion
  153.4 1.2 subtract_divide_fusion.15
  154.6 1.1 constant_dynamic-update-slice_fusion.31
  155.9 0.6 copy-done.35
  156.4 0.0 all-gather.2.cloned.1.call-update
  156.5 1.1 convert_bitcast_fusion.12
  157.6 0.6 multiply_reduce_fusion.1
  158.2 1.1 convert_bitcast_fusion.13
  159.3 60.7 %all-gather.2.cloned.1.call-done = f32[16,2,8192]{2,1,0:T(2,128)} async-done(((f32[16,2,128]{2,1,0:T(2,128)}), f32[16,2,8192]{2,1,0:T(2,128)}) %all-gather.2.cloned.1.call-update) | async-done | bytes 1048592 | tf_op jit(solution)/shard_map/all_gather | solution.py:18
  220.0 1.4 slice_bitcast_fusion.15
  221.5 0.0 copy-done.16
  221.5 0.1 copy-done.18
  221.6 0.9 fusion.93
  222.5 0.1 copy-done.20
  222.6 0.9 fusion.78
  223.4 0.9 multiply_reduce_fusion
  224.3 0.8 subtract_bitcast_fusion
  225.1 9.1 %all-reduce = (f32[8]{0:T(128)S(1)}, f32[]{:T(128)}) all-reduce(f32[8]{0:T(128)S(1)} %get-tuple-element.65, f32[]{:T(128)} %multiply_reduce_fusion.1), channel_id=1, replica_groups=mesh['seg_0'=8,'seg_1'=4,'seg_2'=2,'bin'=4] {'bin'}, use_global_device_ids=true, to_apply=%region_36.0 | all-reduce | flops 9 | bytes 72 | tf_op jit(solution)/shard_map/psum | solution.py:160
  234.8 0.5 broadcast_divide_fusion
  (109 shorter events, 0.8 us)
Async XLA Ops:
  7.2 6.7 %copy-start.36 = (s32[8]{0:T(128)S(1)}, s32[8]{0:T(128)}, u32[]{:S(2)}) copy-start(s32[8]{0:T(128)} %param.10) | copy-start | bytes 100
  7.2 6.7 %copy-start.1 = (bf16[8,8,8192]{2,1,0:T(8,128)(2,1)S(1)}, bf16[8,8,8192]{2,1,0:T(8,128)(2,1)}, u32[]{:S(2)}) copy-start(bf16[8,8,8192]{2,1,0:T(8,128)(2,1)} %param.6) | copy-start | bytes 3145732
  7.2 103.2 %reduce-scatter.4.cloned.1.call-start = ((), (), s32[]{:S(2)}) async-start(), calls=%async_computation.3 | async-start | bytes 5898240 | tf_op jit(solution)/shard_map/reduce_scatter | solution.py:12
  13.8 2.3 copy-start.7
  13.8 2.3 copy-start.8
  16.1 3.5 %copy-start.5 = (bf16[8,1,8192]{2,1,0:T(2,128)(2,1)}, bf16[8,1,8192]{2,1,0:T(2,128)(2,1)S(1)}, u32[]{:S(2)}) copy-start(bf16[8,1,8192]{2,1,0:T(2,128)(2,1)S(1)} %get-tuple-element.259) | copy-start | bytes 393220
  16.1 3.5 %copy-start.6 = (bf16[8,1,8192]{2,1,0:T(2,128)(2,1)}, bf16[8,1,8192]{2,1,0:T(2,128)(2,1)S(1)}, u32[]{:S(2)}) copy-start(bf16[8,1,8192]{2,1,0:T(2,128)(2,1)S(1)} %get-tuple-element.260) | copy-start | bytes 393220
  16.1 3.5 %copy-start.9 = (bf16[8,1,8192]{2,1,0:T(2,128)(2,1)}, bf16[8,1,8192]{2,1,0:T(2,128)(2,1)S(1)}, u32[]{:S(2)}) copy-start(bf16[8,1,8192]{2,1,0:T(2,128)(2,1)S(1)} %get-tuple-element.258) | copy-start | bytes 393220
  16.1 3.5 %copy-start.11 = (bf16[8,1,8192]{2,1,0:T(2,128)(2,1)}, bf16[8,1,8192]{2,1,0:T(2,128)(2,1)S(1)}, u32[]{:S(2)}) copy-start(bf16[8,1,8192]{2,1,0:T(2,128)(2,1)S(1)} %get-tuple-element.256) | copy-start | bytes 393220
  16.1 3.5 %copy-start.12 = (bf16[8,1,8192]{2,1,0:T(2,128)(2,1)}, bf16[8,1,8192]{2,1,0:T(2,128)(2,1)S(1)}, u32[]{:S(2)}) copy-start(bf16[8,1,8192]{2,1,0:T(2,128)(2,1)S(1)} %get-tuple-element.262) | copy-start | bytes 393220
  16.1 3.4 %copy-start = (bf16[8,8,8192]{2,1,0:T(8,128)(2,1)S(1)}, bf16[8,8,8192]{2,1,0:T(8,128)(2,1)}, u32[]{:S(2)}) copy-start(bf16[8,8,8192]{2,1,0:T(8,128)(2,1)} %param.7) | copy-start | bytes 3145732
  19.6 7.2 %copy-start.17 = (bf16[8,2,8192]{2,1,0:T(2,128)(2,1)S(1)}, bf16[8,2,8192]{2,1,0:T(2,128)(2,1)}, u32[]{:S(2)}) copy-start(bf16[8,2,8192]{2,1,0:T(2,128)(2,1)} %param.9) | copy-start | bytes 786436
  19.6 7.2 %copy-start.19 = (bf16[8,2,8192]{2,1,0:T(2,128)(2,1)S(1)}, bf16[8,2,8192]{2,1,0:T(2,128)(2,1)}, u32[]{:S(2)}) copy-start(bf16[8,2,8192]{2,1,0:T(2,128)(2,1)} %param.8) | copy-start | bytes 786436
  30.7 0.8 copy-start.33
  33.2 4.2 %copy-start.30 = (f32[8,8192]{1,0:T(8,128)S(1)}, f32[8,8192]{1,0:T(8,128)}, u32[]{:S(2)}) copy-start(f32[8,8192]{1,0:T(8,128)} %get-tuple-element.23) | copy-start | bytes 786436
  33.3 4.2 %copy-start.29 = (f32[8,8192]{1,0:T(8,128)S(1)}, f32[8,8192]{1,0:T(8,128)}, u32[]{:S(2)}) copy-start(f32[8,8192]{1,0:T(8,128)} %get-tuple-element.25) | copy-start | bytes 786436
  33.3 4.3 %copy-start.28 = (f32[8,8192]{1,0:T(8,128)S(1)}, f32[8,8192]{1,0:T(8,128)}, u32[]{:S(2)}) copy-start(f32[8,8192]{1,0:T(8,128)} %get-tuple-element.27) | copy-start | bytes 786436
  33.3 4.3 %copy-start.27 = (f32[8,8192]{1,0:T(8,128)S(1)}, f32[8,8192]{1,0:T(8,128)}, u32[]{:S(2)}) copy-start(f32[8,8192]{1,0:T(8,128)} %get-tuple-element.29) | copy-start | bytes 786436
  33.3 4.3 %copy-start.26 = (f32[8,8192]{1,0:T(8,128)S(1)}, f32[8,8192]{1,0:T(8,128)}, u32[]{:S(2)}) copy-start(f32[8,8192]{1,0:T(8,128)} %get-tuple-element.20) | copy-start | bytes 786436
  34.4 3.3 %copy-start.25 = (f32[8,8192]{1,0:T(8,128)S(1)}, f32[8,8192]{1,0:T(8,128)}, u32[]{:S(2)}) copy-start(f32[8,8192]{1,0:T(8,128)} %get-tuple-element.22) | copy-start | bytes 786436
  35.4 2.3 copy-start.24
  36.4 1.3 copy-start.23
  37.4 1.0 copy-start.22
  37.5 1.0 copy-start.21
  37.5 1.0 copy-start.31
  37.6 1.1 copy-start.32
  41.3 93.1 %reduce-scatter.6.cloned.1.call-start = ((), (), s32[]{:S(2)}) async-start(), calls=%async_computation.4 | async-start | bytes 819200 | tf_op jit(solution)/shard_map/reduce_scatter | solution.py:12
  41.3 2.0 copy-start.10
  110.4 47.2 %copy-start.34 = (f32[8192]{0:T(1024)S(1)}, f32[8192]{0:T(1024)}, u32[]{:S(2)}) copy-start(f32[8192]{0:T(1024)} %param.11) | copy-start | bytes 98308
  110.4 41.7 %reduce-scatter.8.cloned.1.call-start = ((), (), s32[]{:S(2)}) async-start(), calls=%async_computation.5 | async-start | bytes 245760 | tf_op jit(solution)/shard_map/reduce_scatter | solution.py:12
  134.4 85.6 %all-gather.2.cloned.1.call-start = ((), (), s32[]{:S(2)}) async-start(), calls=%async_computation.6 | async-start | bytes 1064960 | tf_op jit(solution)/shard_map/all_gather | solution.py:18
  155.9 0.6 copy-start.35
  157.6 63.8 %copy-start.2 = (f32[8,8192]{1,0:T(8,128)S(1)}, f32[8,8192]{1,0:T(8,128)}, u32[]{:S(2)}) copy-start(f32[8,8192]{1,0:T(8,128)} %get-tuple-element.289) | copy-start | bytes 786436
  157.6 63.8 %copy-start.3 = (f32[8,8192]{1,0:T(8,128)S(1)}, f32[8,8192]{1,0:T(8,128)}, u32[]{:S(2)}) copy-start(f32[8,8192]{1,0:T(8,128)} %get-tuple-element.296) | copy-start | bytes 786436
  159.3 62.1 %copy-start.4 = (f32[8,8192]{1,0:T(8,128)S(1)}, f32[8,8192]{1,0:T(8,128)}, u32[]{:S(2)}) copy-start(f32[8,8192]{1,0:T(8,128)} %get-tuple-element.297) | copy-start | bytes 786436
  159.3 62.1 %copy-start.13 = (f32[8,8192]{1,0:T(8,128)S(1)}, f32[8,8192]{1,0:T(8,128)}, u32[]{:S(2)}) copy-start(f32[8,8192]{1,0:T(8,128)} %get-tuple-element.290) | copy-start | bytes 786436
  220.0 1.4 copy-start.14
  220.0 1.5 copy-start.15
  220.0 1.5 copy-start.16
  220.0 1.6 copy-start.18
  221.6 0.9 copy-start.20
Sparse Core Ops, SparseCore 0:
  41.4 68.9 reduce-scatter.3
  112.9 21.4 reduce-scatter.5
  136.9 15.2 reduce-scatter.7
  156.6 63.3 all-gather.1
where the time goes:
time: 243 us; the launch traced here: 242 us
  waiting for transfers between devices  165 us (68%)
  other arithmetic  32.5 us (13%)
  local copies, waits for them, and re-layouts  20 us (8%)
  between operations  15.3 us (6%)
  blocking collectives  9.06 us (4%)
    reduce_scatter x3, waiting for transfers between devices, summed_rows(): shard = lax.psum_scatter(shard, axis, scatter_dimension=dim, tiled=True)  104 us
    all_gather x1, waiting for transfers between devices, sent_together(): lax.all_gather(both, axis, axis=dim, tiled=True)  60.7 us
    psum x1, blocking collectives, on_device(): summed, norm_square = lax.psum((numerator, weight_square), 'bin')  9.06 us
    unnamed x116, local copies, waits for them, and re-layouts  7.14 us
    reduce_sum x1, other arithmetic, cross_spectra(): jnp.sum(left_real * magnet_real.astype(jnp.float32) + left_imag * magnet_...  7.14 us
    slice x1, local copies, waits for them, and re-layouts, cross_spectra(): left_imag = (magnet_imag[:, chan].astype(jnp.float32) * keep)[:, None, :]  6.59 us
    mul x4, other arithmetic, on_device(): weight_real * field_real  4.91 us
  transfers between devices with their start and end apart: 4, of which 4 were waited for; matrix products, arithmetic and copies ran while one was open for 4% of the time, Pallas kernels for 0%

commit v1 on v0

v1 whole, which is shorter than its diff:
```python
import jax
import jax.numpy as jnp
from jax import lax
from jax.experimental import pallas as pl
from jax.experimental.pallas import tpu as pltpu
from jax.sharding import Mesh
from jax.sharding import PartitionSpec as P

SEG = ("seg_0", "seg_1", "seg_2")
MESH = pl.DeviceIdType.MESH
F32 = jnp.float32
NZ, NX, NY = 8, 4, 4
LANES = 128
SEGS = 8
ROWS = 96
WROWS = 32
TILES = 64

ORDER0 = ((2, 0), (2, 1), (1, 1), (3, 0), (1, 0), (3, 1), (0, 0), (0, 1))
ORDER1 = (4, 3, 5, 2, 6, 1, 7, 0)


def row_ids():
    return lax.broadcasted_iota(jnp.int32, (8, LANES), 0)


def spread(a, j):
    return jnp.broadcast_to(a[j : j + 1, :], (8, LANES))


def spectra_tile(tile, mr, mi, dr, di, keep, hbuf, put):
    lanes = pl.ds(pl.multiple_of(tile * LANES, LANES), LANES)
    rows = row_ids()
    total = [jnp.zeros((8, LANES), F32) for _ in range(13)]
    held = [jnp.zeros((8, LANES), F32) for _ in range(4)]
    for s in range(SEGS):
        a = mr[s, :, lanes].astype(F32)
        b = mi[s, :, lanes].astype(F32)
        hr = dr[s, :, lanes].astype(F32)
        hi = di[s, :, lanes].astype(F32)
        v = keep[s]
        ka, kb = a * v, b * v
        total[0] += ka * a + kb * b
        for r in range(1, 5):
            ra, rb = pltpu.roll(a, 8 - r, 0), pltpu.roll(b, 8 - r, 0)
            total[2 * r - 1] += ka * ra + kb * rb
            total[2 * r] += kb * ra - ka * rb
        for k in range(2):
            pr, pi = spread(hr, k), spread(hi, k)
            total[9 + 2 * k] += ka * pr + kb * pi
            total[10 + 2 * k] += kb * pr - ka * pi
            held[2 * k] = jnp.where(rows == s, pr, held[2 * k])
            held[2 * k + 1] = jnp.where(rows == s, pi, held[2 * k + 1])
    total[7] = jnp.where(rows < 4, total[7], total[8])
    del total[8]
    for q in range(12):
        put(q, total[q])
    for q in range(4):
        hbuf[tile, 8 * q : 8 * q + 8, :] = held[q]


def solve(spec):
    rows = row_ids()
    re, im = [None] * 8, [None] * 8
    re[0], im[0] = spec[0], jnp.zeros((8, LANES), F32)
    for r in (1, 2, 3):
        re[r], im[r] = spec[2 * r - 1], spec[2 * r]
        re[8 - r] = pltpu.roll(re[r], r, 0)
        im[8 - r] = -pltpu.roll(im[r], r, 0)
    turned = pltpu.roll(spec[7], 4, 0)
    re[4] = jnp.where(rows < 4, spec[7], turned)
    im[4] = jnp.where(rows < 4, -turned, spec[7])
    cr, ci = [], []
    for d in range(8):
        a, b = re[d], im[d]
        for c in range(1, 8):
            a = jnp.where(rows == c, re[(d - c) % 8], a)
            b = jnp.where(rows == c, im[(d - c) % 8], b)
        cr.append(jnp.where(rows == d, a + 1.0, a))
        ci.append(b)
    cr += [spec[8], spec[10]]
    ci += [spec[9], spec[11]]
    inverse = []
    for j in range(8):
        inverse.append(1.0 / spread(cr[j], j))
        fr = jnp.where(rows > j, cr[j] * inverse[j], 0.0)
        fi = jnp.where(rows > j, ci[j] * inverse[j], 0.0)
        for d in range(j + 1, 10):
            pr, pi = spread(cr[d], j), spread(ci[d], j)
            cr[d] = cr[d] - (fr * pr - fi * pi)
            ci[d] = ci[d] - (fr * pi + fi * pr)
    out = []
    for k in (8, 9):
        yr, yi = cr[k], ci[k]
        wr, wi = jnp.zeros((8, LANES), F32), jnp.zeros((8, LANES), F32)
        for d in reversed(range(8)):
            xr, xi = spread(yr, d) * inverse[d], spread(yi, d) * inverse[d]
            wr = jnp.where(rows == d, xr, wr)
            wi = jnp.where(rows == d, xi, wi)
            yr = yr - (cr[d] * xr - ci[d] * xi)
            yi = yi - (cr[d] * xi + ci[d] * xr)
        out += [wr, wi]
    return out


def row_sums(parts):
    rows = row_ids()
    low = rows < 4
    merged = []
    for s in range(4):
        a, b = parts[s], parts[s + 4]
        merged.append(jnp.where(low, a, b) + pltpu.roll(jnp.where(low, b, a), 4, 0))
    for step in (2, 1):
        first = (rows & step) == 0
        merged = [
            jnp.where(
                first,
                merged[s] + pltpu.roll(merged[s], 8 - step, 0),
                merged[s + step] + pltpu.roll(merged[s + step], step, 0),
            )
            for s in range(step)
        ]
    return merged[0]


def clean_tile(tile, mr, mi, inter, wbuf, hbuf, out_r, out_i):
    lanes = pl.ds(pl.multiple_of(tile * LANES, LANES), LANES)
    w = [wbuf[tile, 8 * q : 8 * q + 8, :] for q in range(4)]
    parts = [[], [], [], []]
    for s in range(SEGS):
        a = mr[s, :, lanes].astype(F32)
        b = mi[s, :, lanes].astype(F32)
        for k in range(2):
            parts[2 * k].append(w[2 * k] * a + w[2 * k + 1] * b)
            parts[2 * k + 1].append(w[2 * k] * b - w[2 * k + 1] * a)
    g = [hbuf[tile, 8 * q : 8 * q + 8, :] - row_sums(parts[q]) for q in range(4)]
    real = g[0] * g[2] + g[1] * g[3]
    out_r[:, lanes] = real
    out_i[:, lanes] = g[1] * g[2] - g[0] * g[3]
    return real * inter[pl.ds(tile, 1), :]


def kernel(
    mr, mi, dr, di, keep, inter, out_r, out_i, est,
    acc, outbox, inbox, rbuf, pbuf, wbuf, hbuf, num, ybuf,
    p_send, p_recv, r_send, r_recv, q_send, q_recv, z_send, z_recv,
    x_send, x_recv, f_send, f_recv, w_send, w_recv, y_send, y_recv,
):
    z, x, c = lax.axis_index("seg_0"), lax.axis_index("seg_1"), lax.axis_index("seg_2")
    y = lax.axis_index("bin")

    def at_z(d):
        return {"seg_0": lax.rem(z + d, NZ)}

    def at_x(d):
        return {"seg_1": lax.rem(x + d, NX)}

    def at_y(d):
        return {"bin": lax.rem(y + d, NY)}

    partner = {"seg_2": 1 - c}

    barrier = pltpu.get_barrier_semaphore()
    peers = [at_z(d) for d in range(1, NZ)] + [at_x(d) for d in range(1, NX)]
    peers += [at_y(d) for d in range(1, NY)] + [partner]
    for peer in peers:
        pl.semaphore_signal(barrier, inc=1, device_id=peer, device_id_type=MESH)

    def copy(src, dst, send, recv, where):
        return pltpu.make_async_remote_copy(
            src_ref=src, dst_ref=dst, send_sem=send, recv_sem=recv,
            device_id=where, device_id_type=MESH,
        )

    def add_into(dst, at, src, first, count):
        def body(i, carry):
            for q in range(12):
                block = pl.ds(8 * q, 8)
                dst[at + i, block, :] = dst[at + i, block, :] + src[first + i, block, :]
            return carry

        lax.fori_loop(0, count, body, 0)

    on_core0 = c == 0

    def first_tiles(g):
        d, half = ORDER0[g]
        zero = lax.rem(x + d, NX) * 8 + 4 * half
        one = 32 + lax.rem(z + ORDER1[g], NZ) * 4
        return jnp.where(on_core0, zero, one), jnp.where(on_core0, one, zero)

    def make_group(g, tile, dst):
        def body(i, carry):
            def put(q, value):
                dst[4 * g + i, 8 * q : 8 * q + 8, :] = value

            spectra_tile(tile + i, mr, mi, dr, di, keep, hbuf, put)
            return carry

        lax.fori_loop(0, 4, body, 0)

    to_partner = [
        copy(outbox.at[pl.ds(4 * g, 4)], inbox.at[pl.ds(4 * g, 4)],
             p_send.at[g], p_recv.at[g], partner)
        for g in range(8)
    ]

    def hop(first, count, place, slot, way):
        where = {0: (at_x(1), at_x(3)), 1: (at_z(1), at_z(7))}[way // 2][way % 2]
        return copy(acc.at[pl.ds(first, count)], rbuf.at[pl.ds(place, count)],
                    r_send.at[slot], r_recv.at[slot], where)

    zero_hops = [
        [hop(0, 4, 0, 0, 0), hop(8, 4, 4, 1, 0), hop(16, 4, 8, 2, 0)],
        [hop(4, 4, 12, 3, 1), hop(12, 4, 16, 4, 1), hop(20, 4, 20, 5, 1)],
    ]
    up = [0, 6, 4, 14, 12, 22, 20]
    down = [2, 8, 10, 16, 18, 24, 26]
    one_hops = [
        [hop(up[m], 2, 2 * m, m, 2) for m in range(7)],
        [hop(down[m], 2, 14 + 2 * m, 7 + m, 3) for m in range(7)],
    ]

    def combine(g):
        to_partner[g].wait_recv()
        add_into(acc, 4 * g, inbox, 4 * g, 4)
        if g < 4:

            @pl.when(on_core0)
            def _():
                zero_hops[g % 2][g // 2].start()

        @pl.when(jnp.logical_not(on_core0))
        def _():
            if g == 0:
                one_hops[0][0].start()
                one_hops[1][0].start()
            if g == 1:
                one_hops[0][1].start()
            if g == 2:
                one_hops[1][1].start()

    for g in range(8):
        own, other = first_tiles(g)
        make_group(g, other, outbox)
        if g == 0:
            pl.semaphore_wait(barrier, len(peers))
        to_partner[g].start()
        make_group(g, own, acc)
        if g:
            combine(g - 1)
    combine(7)

    spec_at = jnp.where(on_core0, 24 + z, 28 + x)
    far_first = (4, 3, 5, 2, 6, 1, 7)
    zero_last = {
        d: copy(acc.at[24 + lax.rem(z + d, NZ)], pbuf.at[d], q_send.at[d], q_recv.at[d], at_z(d))
        for d in far_first
    }
    one_last = {
        d: copy(acc.at[28 + lax.rem(x + d, NX)], pbuf.at[d], q_send.at[d], q_recv.at[d], at_x(d))
        for d in (2, 1, 3)
    }

    @pl.when(on_core0)
    def _():
        for way in range(2):
            first, _, last = zero_hops[way]
            first.wait_recv()
            add_into(acc, 16 + 4 * way, rbuf, 12 * way, 4)
            last.start()
        for way in range(2):
            zero_hops[way][1].wait_recv()
            add_into(acc, 28 - 4 * way, rbuf, 4 + 12 * way, 4)
        for way in range(2):
            zero_hops[way][2].wait_recv()
            add_into(acc, 24 + 4 * way, rbuf, 8 + 12 * way, 4)
        for d in far_first:
            zero_last[d].start()
        for d in reversed(far_first):
            zero_last[d].wait_recv()
            add_into(acc, spec_at, pbuf, d, 1)

    @pl.when(jnp.logical_not(on_core0))
    def _():
        for m in range(7):
            for way in range(2):
                chunks = (up, down)[way]
                target = chunks[2] if m == 0 else (chunks[m + 2] if m < 5 else None)
                if target is None:
                    target = ((30, 28), (28, 30))[way][m - 5]
                one_hops[way][m].wait_recv()
                add_into(acc, target, rbuf, 14 * way + 2 * m, 2)
                if m < 5:
                    one_hops[way][m + 2].start()
        for d in (2, 1, 3):
            one_last[d].start()
        for d in (1, 3, 2):
            one_last[d].wait_recv()
            add_into(acc, spec_at, pbuf, d, 1)

    spec = [acc[spec_at, 8 * q : 8 * q + 8, :] for q in range(12)]
    filters = solve(spec)

    def tile_of(core, zz, xx):
        return jnp.where(core == 0, xx * 8 + zz, 32 + zz * 4 + xx)

    mine = tile_of(c, z, x)
    for q in range(4):
        wbuf[mine, 8 * q : 8 * q + 8, :] = filters[q]

    def w_copy(tile, send, recv, where):
        return copy(wbuf.at[tile], wbuf.at[tile], send, recv, where)

    along_z = {d: w_copy(mine, z_send.at[d], z_recv.at[d], at_z(d)) for d in far_first}
    for d in far_first:
        along_z[d].start()

    square = inter[0:8, :] * inter[0:8, :]
    for i in range(1, 8):
        square = square + inter[8 * i : 8 * i + 8, :] * inter[8 * i : 8 * i + 8, :]
    num[...] = jnp.zeros_like(num)

    def z_of(d):
        return lax.rem(z + NZ - d, NZ)

    def x_of(d):
        return lax.rem(x + NX - d, NX)

    def tile_from(core, dz, dx):
        return tile_of(core, z_of(dz), x_of(dx))

    def got(tile, sem, where):
        w_copy(tile, z_send.at[0], sem, where).wait_recv()

    def cleaned(tile):
        num[...] += clean_tile(tile, mr, mi, inter, wbuf, hbuf, out_r, out_i)

    near_first = (0, 1, 7, 2, 6, 3, 5, 4)
    sent = []

    def share(kind, d, tile):
        to_core = w_copy(tile, w_send.at[kind, d], w_recv.at[kind, d], partner)
        to_core.start()
        sent.append(to_core)

    for d in near_first:
        tile = tile_from(c, d, 0)
        if d:
            got(tile, z_recv.at[d], at_z(NZ - d))
        for way, dx in ((0, 1), (1, 3)):
            onward = w_copy(tile, x_send.at[way, d], x_recv.at[way, d], at_x(dx))
            onward.start()
            sent.append(onward)
        share(0, d, tile)
        cleaned(tile)
    for d in near_first:
        for way, dx in ((0, 1), (1, 3)):
            tile = tile_from(c, d, dx)
            got(tile, x_recv.at[way, d], at_x(NX - dx))
            if way == (near_first.index(d) % 2):
                onward = w_copy(tile, f_send.at[d], f_recv.at[d], at_x(dx))
                onward.start()
                sent.append(onward)
            share(dx, d, tile)
            cleaned(tile)
    for d in near_first:
        tile = tile_from(c, d, 2)
        got(tile, f_recv.at[d], at_x(1 if near_first.index(d) % 2 == 1 else 3))
        share(2, d, tile)
    for dx in (0, 1, 3):
        for d in near_first:
            tile = tile_from(1 - c, d, dx)
            got(tile, w_recv.at[dx, d], partner)
            cleaned(tile)
    for d in near_first:
        cleaned(tile_from(c, d, 2))
    for d in near_first:
        tile = tile_from(1 - c, d, 2)
        got(tile, w_recv.at[2, d], partner)
        cleaned(tile)

    ybuf[y, 0:8, :] = num[...]
    ybuf[y, 8:16, :] = square
    over_y = [
        copy(ybuf.at[y], ybuf.at[y], y_send.at[d], y_recv.at[d], at_y(d)) for d in range(1, NY)
    ]
    for step in over_y:
        step.start()
    for d in range(1, NY):
        src = lax.rem(y + NY - d, NY)
        copy(ybuf.at[src], ybuf.at[src], y_send.at[d], y_recv.at[d], at_y(NY - d)).wait_recv()
    top, norm = ybuf[0, 0:8, :], ybuf[0, 8:16, :]
    for i in range(1, NY):
        top, norm = top + ybuf[i, 0:8, :], norm + ybuf[i, 8:16, :]
    top = jnp.sum(top, axis=1, keepdims=True)
    norm = jnp.sum(jnp.sum(norm, axis=1, keepdims=True), axis=0, keepdims=True)
    value = jnp.broadcast_to(top / jnp.sqrt(norm), (8, LANES))
    diagonal = row_ids() == lax.broadcasted_iota(jnp.int32, (8, LANES), 1)
    est[...] = jnp.sum(jnp.where(diagonal, value, 0.0), axis=0, keepdims=True)

    for step in over_y + sent + [along_z[d] for d in far_first] + to_partner:
        step.wait_send()

    @pl.when(on_core0)
    def _():
        for step in zero_hops[0] + zero_hops[1] + [zero_last[d] for d in far_first]:
            step.wait_send()

    @pl.when(jnp.logical_not(on_core0))
    def _():
        for step in one_hops[0] + one_hops[1] + [one_last[d] for d in (2, 1, 3)]:
            step.wait_send()


def on_device(magnet_real, magnet_imag, detector_real, detector_imag, valid, intersection):
    bins = magnet_real.shape[2]
    assert bins == TILES * LANES and magnet_real.shape[:2] == (SEGS, 8)
    dma = pltpu.SemaphoreType.DMA
    vmem = pl.BlockSpec(memory_space=pltpu.VMEM)
    smem = pl.BlockSpec(memory_space=pltpu.SMEM)
    cleaned_real, cleaned_imag, estimate = pl.pallas_call(
        kernel,
        out_shape=(
            jax.ShapeDtypeStruct((SEGS, bins), F32),
            jax.ShapeDtypeStruct((SEGS, bins), F32),
            jax.ShapeDtypeStruct((1, LANES), F32),
        ),
        in_specs=[vmem, vmem, vmem, vmem, smem, vmem],
        out_specs=(vmem, vmem, vmem),
        scratch_shapes=[
            pltpu.VMEM((32, ROWS, LANES), F32),
            pltpu.VMEM((32, ROWS, LANES), F32),
            pltpu.VMEM((32, ROWS, LANES), F32),
            pltpu.VMEM((28, ROWS, LANES), F32),
            pltpu.VMEM((8, ROWS, LANES), F32),
            pltpu.VMEM((TILES, WROWS, LANES), F32),
            pltpu.VMEM((TILES, 32, LANES), F32),
            pltpu.VMEM((8, LANES), F32),
            pltpu.VMEM((NY, 16, LANES), F32),
            dma((8,)), dma((8,)), dma((14,)), dma((14,)), dma((8,)), dma((8,)),
            dma((8,)), dma((8,)), dma((2, 8)), dma((2, 8)), dma((8,)), dma((8,)),
            dma((4, 8)), dma((4, 8)), dma((4,)), dma((4,)),
        ],
        compiler_params=pltpu.CompilerParams(collective_id=0, has_side_effects=True),
    )(
        magnet_real, magnet_imag, detector_real, detector_imag,
        valid.astype(F32), intersection.reshape(TILES, LANES),
    )
    return cleaned_real, cleaned_imag, estimate[0, :SEGS]


def solution(mesh):
    assert mesh.shape["seg"] == NZ * NX * 2 and mesh.shape["bin"] == NY
    torus = Mesh(mesh.devices.reshape(NZ, NX, 2, NY), ("seg_0", "seg_1", "seg_2", "bin"))
    spec3 = P(SEG, None, "bin")
    return jax.shard_map(
        on_device, mesh=torus,
        in_specs=(spec3, spec3, spec3, spec3, P(SEG), P("bin")),
        out_specs=(P(SEG, "bin"), P(SEG, "bin"), P(SEG)),
        check_vma=False,
    )
```

time: 243 us -> 57.4 us (0.24)
  waiting for transfers between devices: 165 us -> 0 us
  Pallas kernels: 0 us -> 51.9 us
  other arithmetic: 32.5 us -> 0.51 us
  local copies, waits for them, and re-layouts: 20 us -> 4.17 us
  between operations: 15.3 us -> 0.66 us
  blocking collectives: 9.06 us -> 0 us
    reduce_scatter x3 -> x0, waiting for transfers between devices: 104 us -> none  [summed_rows(): shard = lax.psum_scatter(shard, axis, scatter_dimension=dim, tiled=True)]
    all_gather x1 -> x0, waiting for transfers between devices: 60.7 us -> none  [sent_together(): lax.all_gather(both, axis, axis=dim, tiled=True)]
    pallas_call x0 -> x1, Pallas kernels: none -> 51.9 us  [on_device(): pl.pallas_call(kernel, out_shape=(jax.ShapeDtypeStruct((SEGS, bins), F32)...]
    reduce_sum x4 -> x0, other arithmetic: 12.3 us -> none  [the longest x1 7.14 us: cross_spectra(): jnp.sum(left_real * magnet_real.astype(jnp.float32) + left_imag * magnet_...]
    mul x9 -> x0, other arithmetic: 12.1 us -> none  [the longest x4 4.91 us: on_device(): weight_real * field_real]
    psum x1 -> x0, blocking collectives: 9.06 us -> none  [on_device(): summed, norm_square = lax.psum((numerator, weight_square), 'bin')]
    slice x2 -> x0, local copies, waits for them, and re-layouts: 8.76 us -> none  [the longest x1 6.59 us: cross_spectra(): left_imag = (magnet_imag[:, chan].astype(jnp.float32) * keep)[:, None, :]]
    unnamed x116 -> x8, local copies, waits for them, and re-layouts: 7.14 us -> 3.65 us
  transfers between devices with their start and end apart: 4 -> 0, of which waited for: 4 -> 0; matrix products, arithmetic and copies ran while one was open for 4% -> 0% of each run, Pallas kernels for 0% -> 0%
where the time goes in v1:
time: 57.4 us; the launch traced here: 57.2 us
  Pallas kernels  51.9 us (90%)
  local copies, waits for them, and re-layouts  4.17 us (7%)
  between operations  0.66 us (1%)
    pallas_call x1, Pallas kernels, on_device(): pl.pallas_call(kernel, out_shape=(jax.ShapeDtypeStruct((SEGS, bins), F32)...  51.9 us
    unnamed x8, local copies, waits for them, and re-layouts  3.65 us

profile of v1, /device:TPU:1, one launch (start us, length us, event | category | flops | bytes accessed | tf_op | source)
XLA Modules:
  0.0 57.2 jit_solution(17039039560892396294)
XLA Ops:
  0.6 0.0 copy-start.1
  0.6 0.6 %copy-done.1 = s32[8]{0:T(128)S(1)} copy-done((s32[8]{0:T(128)S(1)}, s32[8]{0:T(128)}, u32[]{:S(2)}) %copy-start.1) | copy-done | bytes 56
  1.3 0.5 convert_element_type.3.keep
  1.8 51.9 %shard_map.85 = (f32[8,8192]{1,0:T(8,128)}, f32[8,8192]{1,0:T(8,128)}, f32[1,128]{1,0:T(1,128)}) custom-call(bf16[8,8,8192]{2,1,0:T(8,128)(2,1)} %mr.1, bf16[8,8,8192]{2,1,0:T(8,128)(2,1)} %mi.1, bf16[8,2,8192]{2,1,0:T(2,128)(2,1)} %dr.1, bf16[8,2,8192]{2,1,0:T(2,128)(2,1)} %di.1, f32[8]{0:T(128)} %convert_element_type.3.keep, f32[64,128]{1,0:T(8,128)} %bitcast.3), custom_call_target="tpu_custom_call" | custom-call | tf_op jit(solution)/shard_map/pallas_call | solution.py:422
  53.7 0.0 copy-start.2
  53.7 0.6 %copy-done.2 = f32[1,128]{1,0:T(1,128)S(1)} copy-done((f32[1,128]{1,0:T(1,128)S(1)}, f32[1,128]{1,0:T(1,128)}, u32[]{:S(2)}) %copy-start.2) | copy-done | bytes 536
  54.3 0.5 slice_bitcast_fusion
  54.8 0.0 copy-start
  54.8 1.7 %copy.11 = f32[8,8192]{1,0:T(8,128)} copy(f32[8,8192]{1,0:T(8,128)} %get-tuple-element.12) | data formatting | bytes 524288
  56.5 0.0 copy-done
  56.5 0.7 %copy.12 = f32[8,8192]{1,0:T(8,128)} copy(f32[8,8192]{1,0:T(8,128)S(1)} %copy-done) | data formatting | bytes 524288
Async XLA Ops:
  0.6 0.7 %copy-start.1 = (s32[8]{0:T(128)S(1)}, s32[8]{0:T(128)}, u32[]{:S(2)}) copy-start(s32[8]{0:T(128)} %param.10) | copy-start | bytes 100
  53.7 0.6 %copy-start.2 = (f32[1,128]{1,0:T(1,128)S(1)}, f32[1,128]{1,0:T(1,128)}, u32[]{:S(2)}) copy-start(f32[1,128]{1,0:T(1,128)} %get-tuple-element.8) | copy-start | bytes 1540
  54.8 1.7 %copy-start = (f32[8,8192]{1,0:T(8,128)S(1)}, f32[8,8192]{1,0:T(8,128)}, u32[]{:S(2)}) copy-start(f32[8,8192]{1,0:T(8,128)} %get-tuple-element.13) | copy-start | bytes 786436

commit v2 on v1

v2 whole, which is shorter than its diff:
```python
import jax
import jax.numpy as jnp
from jax import lax
from jax.experimental import pallas as pl
from jax.experimental.pallas import tpu as pltpu
from jax.sharding import Mesh
from jax.sharding import PartitionSpec as P

SEG = ("seg_0", "seg_1", "seg_2")
MESH = pl.DeviceIdType.MESH
F32 = jnp.float32
NZ, NX, NY = 8, 4, 4
LANES = 128
SEGS = 8
ROWS = 96
WROWS = 32
TILES = 64

ORDER0 = ((2, 0), (2, 1), (1, 1), (3, 0), (1, 0), (3, 1), (0, 0), (0, 1))
ORDER1 = (4, 3, 5, 2, 6, 1, 7, 0)
HALVES0 = ((4, 3, 2, 1), (5, 7, 6, 0))
INSIDE1 = (2, 1, 3, 0)
LAST = 31


def row_ids():
    return lax.broadcasted_iota(jnp.int32, (8, LANES), 0)


def spread(a, j):
    return jnp.broadcast_to(a[j : j + 1, :], (8, LANES))


def spectra_tile(tile, mr, mi, dr, di, keep, hbuf, put):
    lanes = pl.ds(pl.multiple_of(tile * LANES, LANES), LANES)
    rows = row_ids()
    total = [jnp.zeros((8, LANES), F32) for _ in range(13)]
    held = [jnp.zeros((8, LANES), F32) for _ in range(4)]
    for s in range(SEGS):
        a = mr[s, :, lanes].astype(F32)
        b = mi[s, :, lanes].astype(F32)
        hr = dr[s, :, lanes].astype(F32)
        hi = di[s, :, lanes].astype(F32)
        v = keep[s].astype(F32)
        ka, kb = a * v, b * v
        total[0] += ka * a + kb * b
        for r in range(1, 5):
            ra, rb = pltpu.roll(a, 8 - r, 0), pltpu.roll(b, 8 - r, 0)
            total[2 * r - 1] += ka * ra + kb * rb
            total[2 * r] += kb * ra - ka * rb
        for k in range(2):
            pr, pi = spread(hr, k), spread(hi, k)
            total[9 + 2 * k] += ka * pr + kb * pi
            total[10 + 2 * k] += kb * pr - ka * pi
            held[2 * k] = jnp.where(rows == s, pr, held[2 * k])
            held[2 * k + 1] = jnp.where(rows == s, pi, held[2 * k + 1])
    total[7] = jnp.where(rows < 4, total[7], total[8])
    del total[8]
    for q in range(12):
        put(q, total[q])
    for q in range(4):
        hbuf[tile, 8 * q : 8 * q + 8, :] = held[q]


def solve(spec):
    rows = row_ids()
    re, im = [None] * 8, [None] * 8
    re[0], im[0] = spec[0], jnp.zeros((8, LANES), F32)
    for r in (1, 2, 3):
        re[r], im[r] = spec[2 * r - 1], spec[2 * r]
        re[8 - r] = pltpu.roll(re[r], r, 0)
        im[8 - r] = -pltpu.roll(im[r], r, 0)
    turned = pltpu.roll(spec[7], 4, 0)
    re[4] = jnp.where(rows < 4, spec[7], turned)
    im[4] = jnp.where(rows < 4, -turned, spec[7])
    cr, ci = [], []
    for d in range(8):
        a, b = re[d], im[d]
        for c in range(1, 8):
            a = jnp.where(rows == c, re[(d - c) % 8], a)
            b = jnp.where(rows == c, im[(d - c) % 8], b)
        cr.append(jnp.where(rows == d, a + 1.0, a))
        ci.append(b)
    cr += [spec[8], spec[10]]
    ci += [spec[9], spec[11]]
    inverse = []
    for j in range(8):
        inverse.append(1.0 / spread(cr[j], j))
        fr = jnp.where(rows > j, cr[j] * inverse[j], 0.0)
        fi = jnp.where(rows > j, ci[j] * inverse[j], 0.0)
        for d in range(j + 1, 10):
            pr, pi = spread(cr[d], j), spread(ci[d], j)
            cr[d] = cr[d] - (fr * pr - fi * pi)
            ci[d] = ci[d] - (fr * pi + fi * pr)
    out = []
    for k in (8, 9):
        yr, yi = cr[k], ci[k]
        wr, wi = jnp.zeros((8, LANES), F32), jnp.zeros((8, LANES), F32)
        for d in reversed(range(8)):
            xr, xi = spread(yr, d) * inverse[d], spread(yi, d) * inverse[d]
            wr = jnp.where(rows == d, xr, wr)
            wi = jnp.where(rows == d, xi, wi)
            yr = yr - (cr[d] * xr - ci[d] * xi)
            yi = yi - (cr[d] * xi + ci[d] * xr)
        out += [wr, wi]
    return out


def row_sums(parts):
    rows = row_ids()
    low = rows < 4
    merged = []
    for s in range(4):
        a, b = parts[s], parts[s + 4]
        merged.append(jnp.where(low, a, b) + pltpu.roll(jnp.where(low, b, a), 4, 0))
    for step in (2, 1):
        first = (rows & step) == 0
        merged = [
            jnp.where(
                first,
                merged[s] + pltpu.roll(merged[s], 8 - step, 0),
                merged[s + step] + pltpu.roll(merged[s + step], step, 0),
            )
            for s in range(step)
        ]
    return merged[0]


def clean_tile(tile, mr, mi, inter, wbuf, hbuf, out_r, out_i):
    lanes = pl.ds(pl.multiple_of(tile * LANES, LANES), LANES)
    w = [wbuf[tile, 8 * q : 8 * q + 8, :] for q in range(4)]
    parts = [[], [], [], []]
    for s in range(SEGS):
        a = mr[s, :, lanes].astype(F32)
        b = mi[s, :, lanes].astype(F32)
        for k in range(2):
            parts[2 * k].append(w[2 * k] * a + w[2 * k + 1] * b)
            parts[2 * k + 1].append(w[2 * k] * b - w[2 * k + 1] * a)
    g = [hbuf[tile, 8 * q : 8 * q + 8, :] - row_sums(parts[q]) for q in range(4)]
    real = g[0] * g[2] + g[1] * g[3]
    out_r[:, lanes] = real
    out_i[:, lanes] = g[1] * g[2] - g[0] * g[3]
    return real * inter[pl.ds(tile, 1), :]


def kernel(
    mr_hbm, mi_hbm, dr_hbm, di_hbm, keep_hbm, inter_hbm, out_r, out_i, est,
    mr, mi, dr, di, keep, inter, acc, outbox, inbox, rbuf, pbuf, wbuf, hbuf, num, ybuf,
    m_in, d_in, sent, p_recv, r_recv, q_recv, z_recv, x_recv, f_recv, w_recv, y_recv,
):
    z, x, c = lax.axis_index("seg_0"), lax.axis_index("seg_1"), lax.axis_index("seg_2")
    y = lax.axis_index("bin")

    def at_z(d):
        return {"seg_0": lax.rem(z + d, NZ)}

    def at_x(d):
        return {"seg_1": lax.rem(x + d, NX)}

    def at_y(d):
        return {"bin": lax.rem(y + d, NY)}

    partner = {"seg_2": 1 - c}

    barrier = pltpu.get_barrier_semaphore()
    peers = [at_z(d) for d in (1, 2, 6, 7)] + [at_x(d) for d in range(1, NX)]
    peers += [at_y(d) for d in range(1, NY)] + [partner]
    for peer in peers:
        pl.semaphore_signal(barrier, inc=1, device_id=peer, device_id_type=MESH)

    on_core0 = c == 0

    def tile0(xo, zo):
        return lax.rem(x + xo, NX) * 8 + lax.rem(z + zo, NZ)

    def tile1(zo, xo):
        return 32 + lax.rem(z + zo, NZ) * 4 + lax.rem(x + xo, NX)

    def fetch(src, dst, first, tiles, sem):
        lanes = pl.ds(pl.multiple_of(first * LANES, 4 * LANES), tiles * LANES)
        return pltpu.make_async_copy(src.at[:, :, lanes], dst.at[:, :, lanes], sem)

    class Pair:
        def __init__(self, first, tiles, sem):
            self.parts = [fetch(mr_hbm, mr, first, tiles, sem), fetch(mi_hbm, mi, first, tiles, sem)]
            whole = mr.at[:, :, pl.ds(0, 2 * tiles * LANES)]
            self.both = pltpu.make_async_copy(whole, whole, sem)

        def start(self):
            for part in self.parts:
                part.start()

        def wait(self):
            self.both.wait()

    loads0, loads1 = {}, {}
    for at, xo in enumerate((2, 1, 3, 0)):
        loads0[xo] = Pair(lax.rem(x + xo, NX) * 8, 8, m_in.at[at])
    for at, zo in enumerate(ORDER1):
        loads1[zo] = Pair(32 + lax.rem(z + zo, NZ) * 4, 4, m_in.at[4 + at])
    small = [
        pltpu.make_async_copy(keep_hbm, keep, d_in.at[0]),
        pltpu.make_async_copy(dr_hbm, dr, d_in.at[1]),
        pltpu.make_async_copy(di_hbm, di, d_in.at[2]),
        pltpu.make_async_copy(inter_hbm, inter, d_in.at[3]),
    ]
    early = small[:3] + [loads0[2], loads1[4], loads1[3]]
    late = [loads0[1], loads1[5], loads1[2], loads0[3], loads1[6], loads1[1], loads0[0], loads1[7], loads1[0]]
    for load in early:
        load.start()

    def copy(src, dst, send, recv, where):
        return pltpu.make_async_remote_copy(
            src_ref=src, dst_ref=dst, send_sem=send, recv_sem=recv,
            device_id=where, device_id_type=MESH,
        )

    def add_into(dst, at, src, first, count):
        for i in range(count):
            for q in range(12):
                block = pl.ds(8 * q, 8)
                dst[at + i, block, :] = dst[at + i, block, :] + src[first + i, block, :]

    def pick(four, i):
        return jnp.where(i < 2, jnp.where(i == 0, *four[:2]), jnp.where(i == 2, *four[2:]))

    def make_group(g, core0, dst):
        xo, half = ORDER0[g]

        def body(i, carry):
            zo, io = pick(HALVES0[half], i), pick(INSIDE1, i)
            tile = jnp.where(core0, tile0(xo, zo), tile1(ORDER1[g], io))

            def put(q, value):
                dst[4 * g + i, 8 * q : 8 * q + 8, :] = value

            spectra_tile(tile, mr, mi, dr, di, keep, hbuf, put)
            return carry

        lax.fori_loop(0, 4, body, 0)

    to_partner = [
        copy(outbox.at[pl.ds(4 * g, 4)], inbox.at[pl.ds(4 * g, 4)],
             sent.at[0], p_recv.at[g], partner)
        for g in range(8)
    ]

    def hop(first, count, place, slot, where):
        return copy(acc.at[pl.ds(first, count)], rbuf.at[pl.ds(place, count)],
                    sent.at[1], r_recv.at[slot], where)

    zero_at = ((0, 2, 8, 10, 16, 18), (4, 6, 12, 14, 20, 22))
    zero_to = ((16, 18, 28, 30, 24, 26), (20, 22, 24, 26, 28, 30))
    zero_hops = [
        [hop(zero_at[w][m], 2, 12 * w + 2 * m, 12 * w + m, at_x((1, 3)[w])) for m in range(6)]
        for w in range(2)
    ]
    one_far = [
        hop((0, 2)[w], 2, 14 * w, 13 * w, at_z((2, 6)[w])) for w in range(2)
    ]
    inside = ((2, 3, 0, 1), (0, 1, 2, 3))
    levels = ((4, 12, 20, 28), (8, 16, 24, 28))
    one_hops = [
        [
            hop(levels[w][m // 4] + inside[w][m % 4], 1, 14 * w + 2 + m, 13 * w + 1 + m, at_z((1, 7)[w]))
            for m in range(12)
        ]
        for w in range(2)
    ]

    def combine(g):
        with jax.named_scope(f"comb{g}"):
            to_partner[g].wait_recv()
            add_into(acc, 4 * g, inbox, 4 * g, 4)

    def zero_take(m):
        for w in range(2):
            with jax.named_scope(f"zt{m}_{w}"):
                zero_hops[w][m].wait_recv()
                add_into(acc, zero_to[w][m], rbuf, 12 * w + 2 * m, 2)
                if m < 2:
                    zero_hops[w][4 + m].start()

    def far_take():
        for w in range(2):
            with jax.named_scope(f"of_{w}"):
                one_far[w].wait_recv()
                add_into(acc, (12, 18)[w], rbuf, 14 * w, 2)

    def one_take(ms):
        for m in ms:
            for w in range(2):
                with jax.named_scope(f"ot{m}_{w}"):
                    one_hops[w][m].wait_recv()
                    add_into(acc, levels[w][m // 4 + 1] + inside[w][m % 4], rbuf, 14 * w + 2 + m, 1)
                    if m < 8:
                        one_hops[w][m + 4].start()

    def zero_send(w, ms):
        for m in ms:
            zero_hops[w][m].start()

    place0 = {zo: 24 + 4 * h + i for h in range(2) for i, zo in enumerate(HALVES0[h])}

    def last_of(src, dst, slot, where):
        return copy(src, dst, sent.at[2], q_recv.at[slot], where)

    top, low = pl.ds(0, ROWS // 2), pl.ds(ROWS // 2, ROWS // 2)
    via = [
        last_of(acc.at[place0[4], top], pbuf.at[2, top], 0, at_z(2)),
        last_of(acc.at[place0[4], low], pbuf.at[2, low], 1, at_z(6)),
        last_of(acc.at[place0[3]], pbuf.at[0], 2, at_z(1)),
        last_of(acc.at[place0[5]], pbuf.at[1], 3, at_z(7)),
    ]
    zero_last = {
        d: last_of(acc.at[place0[d]], pbuf.at[3 + i], 4 + i, at_z(d)) for i, d in enumerate((1, 7, 2, 6))
    }
    one_last = {
        d: last_of(acc.at[28 + INSIDE1.index(d)], pbuf.at[d], d, at_x(d)) for d in (2, 1, 3)
    }

    def add_rows(at, slot, first, blocks):
        for q in range(blocks):
            block = pl.ds(first + 8 * q, 8)
            acc[at, block, :] = acc[at, block, :] + pbuf[slot, block, :]

    plan0 = {0: (0, (0, 1)), 1: (1, (0, 1)), 2: (0, (2, 3)), 3: (1, (2, 3))}

    def after(g):
        combine(g)

        @pl.when(on_core0)
        def _():
            if g in plan0:
                zero_send(*plan0[g])
            if g == 5:
                zero_take(0)
            if g == 6:
                zero_take(1)

        @pl.when(jnp.logical_not(on_core0))
        def _():
            if g == 0:
                one_far[0].start()
                one_far[1].start()
            if g in (1, 2):
                for m in range(4):
                    one_hops[g - 1][m].start()
            if g == 6:
                one_take((0, 1))
                far_take()
                one_take((2, 3))

    for g in range(8):
        xo, half = ORDER0[g]
        with jax.named_scope(f"load{g}"):
            if g == 0:
                for load in small[:3]:
                    load.wait()
            loads1[ORDER1[g]].wait()
            if (xo, half) in ((2, 0), (1, 1), (3, 0), (0, 0)):
                loads0[xo].wait()
        if g == 0:
            for load in late + small[3:]:
                load.start()
        with jax.named_scope(f"mk_other{g}"):
            make_group(g, jnp.logical_not(on_core0), outbox)
        if g == 0:
            with jax.named_scope("barrier"):
                pl.semaphore_wait(barrier, len(peers))
        with jax.named_scope(f"mk_own{g}"):
            to_partner[g].start()
            make_group(g, on_core0, acc)
        if g:
            after(g - 1)
    after(7)

    @pl.when(on_core0)
    def _():
        zero_take(2)
        zero_take(4)
        for step in via + [zero_last[7]]:
            step.start()
        zero_take(3)
        zero_take(5)
        zero_last[1].start()
        with jax.named_scope("p2_via"):
            via[2].wait_recv()
            add_rows(place0[2], 0, 0, 12)
            via[0].wait_recv()
            add_rows(place0[2], 2, 0, 6)
            zero_last[2].start()
            via[3].wait_recv()
            add_rows(place0[6], 1, 0, 12)
            via[1].wait_recv()
            add_rows(place0[6], 2, ROWS // 2, 6)
            zero_last[6].start()
        for i, d in enumerate((1, 7, 2, 6)):
            with jax.named_scope(f"p2_{d}"):
                zero_last[d].wait_recv()
                add_rows(LAST, 3 + i, 0, 12)

    @pl.when(jnp.logical_not(on_core0))
    def _():
        one_take(range(4, 11))
        one_last[2].start()
        one_last[3].start()
        one_take((11,))
        one_last[1].start()
        for d in (2, 3, 1):
            with jax.named_scope(f"q2_{d}"):
                one_last[d].wait_recv()
                add_rows(LAST, d, 0, 12)

    with jax.named_scope("solve"):
        spec = [acc[LAST, 8 * q : 8 * q + 8, :] for q in range(12)]
        filters = solve(spec)

    def tile_of(core, zz, xx):
        return jnp.where(core == 0, xx * 8 + zz, 32 + zz * 4 + xx)

    mine = tile_of(c, z, x)
    for q in range(4):
        wbuf[mine, 8 * q : 8 * q + 8, :] = filters[q]

    def w_copy(tile, recv, where):
        return copy(wbuf.at[tile], wbuf.at[tile], sent.at[3], recv, where)

    far_first = (4, 3, 5, 2, 6, 1, 7)
    along_z = {d: w_copy(mine, z_recv.at[d - 1], at_z(d)) for d in far_first}
    for d in far_first:
        along_z[d].start()

    small[3].wait()
    square = inter[0:8, :] * inter[0:8, :]
    for i in range(1, 8):
        square = square + inter[8 * i : 8 * i + 8, :] * inter[8 * i : 8 * i + 8, :]
    num[...] = jnp.zeros_like(num)

    def tile_from(core, dz, dx):
        return tile_of(core, lax.rem(z + NZ - dz, NZ), lax.rem(x + NX - dx, NX))

    def got(tile, sem, where):
        w_copy(tile, sem, where).wait_recv()

    def cleaned(tile):
        num[...] += clean_tile(tile, mr, mi, inter, wbuf, hbuf, out_r, out_i)

    near_first = (0, 1, 7, 2, 6, 3, 5, 4)

    blocks = [[(d, 0) for d in near_first[:4]], [(d, 0) for d in near_first[4:]]]
    blocks += [[(d, dx) for d in near_first[4 * i : 4 * i + 4] for dx in (1, 3)] for i in range(2)]
    blocks += [[(d, 2) for d in near_first[2 * i : 2 * i + 2]] for i in range(4)]
    block_of = {item: i for i, block in enumerate(blocks) for item in block}

    def share(d, dx, tile):
        w_copy(tile, w_recv.at[block_of[d, dx]], partner).start()

    def got_block(i):
        with jax.named_scope(f"gp{i}"):
            whole = wbuf.at[pl.ds(0, len(blocks[i]))]
            copy(whole, whole, sent.at[3], w_recv.at[i], partner).wait_recv()

    def clean_block(i, first=0, last=8):
        for d, dx in blocks[i][first:last]:
            cleaned(tile_from(1 - c, d, dx))

    for d in near_first:
        tile = tile_from(c, d, 0)
        if d:
            with jax.named_scope(f"gz{d}"):
                got(tile, z_recv.at[d - 1], at_z(NZ - d))
        for way, dx in ((0, 1), (1, 3)):
            w_copy(tile, x_recv.at[way, d], at_x(dx)).start()
        share(d, 0, tile)
        cleaned(tile)
    for i, d in enumerate(near_first):
        for way, dx in ((0, 1), (1, 3)):
            tile = tile_from(c, d, dx)
            with jax.named_scope(f"gx{d}_{dx}"):
                got(tile, x_recv.at[way, d], at_x(NX - dx))
            if way == i % 2:
                w_copy(tile, f_recv.at[d], at_x(dx)).start()
            share(d, dx, tile)
            cleaned(tile)
    for i, d in enumerate(near_first):
        if i in (0, 1):
            got_block(i)
            clean_block(i)
        if i in (2, 4):
            got_block(i // 2 + 1)
            clean_block(i // 2 + 1, 0, 4)
        if i in (3, 5):
            clean_block(i // 2 + 1, 4, 8)
        tile = tile_from(c, d, 2)
        with jax.named_scope(f"gf{d}"):
            got(tile, f_recv.at[d], at_x(1 if i % 2 == 1 else 3))
        share(d, 2, tile)
        cleaned(tile)
    for i in range(4, 8):
        got_block(i)
        clean_block(i)

    with jax.named_scope("ysum"):
        ybuf[y, 0:8, :] = num[...]
        ybuf[y, 8:16, :] = square
        over_y = [
            copy(ybuf.at[y], ybuf.at[y], sent.at[4], y_recv.at[d - 1], at_y(d)) for d in range(1, NY)
        ]
        for step in over_y:
            step.start()
        for d in range(1, NY):
            src = lax.rem(y + NY - d, NY)
            copy(ybuf.at[src], ybuf.at[src], sent.at[4], y_recv.at[d - 1], at_y(NY - d)).wait_recv()
    top, norm = ybuf[0, 0:8, :], ybuf[0, 8:16, :]
    for i in range(1, NY):
        top, norm = top + ybuf[i, 0:8, :], norm + ybuf[i, 8:16, :]
    top = jnp.sum(top, axis=1, keepdims=True)
    norm = jnp.sum(jnp.sum(norm, axis=1, keepdims=True), axis=0, keepdims=True)
    value = jnp.broadcast_to(top / jnp.sqrt(norm), (8, LANES))
    diagonal = row_ids() == lax.broadcasted_iota(jnp.int32, (8, LANES), 1)
    est[...] = jnp.sum(jnp.where(diagonal, value, 0.0), axis=0, keepdims=True)

    def left(ref, sem):
        copy(ref, ref, sem, z_recv.at[0], partner).wait_send()

    left(acc, sent.at[0])
    left(wbuf.at[pl.ds(0, 63)], sent.at[3])
    left(ybuf.at[pl.ds(0, NY - 1)], sent.at[4])

    @pl.when(on_core0)
    def _():
        left(acc.at[pl.ds(0, 24)], sent.at[1])
        left(acc.at[pl.ds(0, 7)], sent.at[2])

    @pl.when(jnp.logical_not(on_core0))
    def _():
        left(acc.at[pl.ds(0, 28)], sent.at[1])
        left(acc.at[pl.ds(0, 3)], sent.at[2])


def on_device(magnet_real, magnet_imag, detector_real, detector_imag, valid, intersection):
    bins = magnet_real.shape[2]
    assert bins == TILES * LANES and magnet_real.shape[:2] == (SEGS, 8)
    dma = pltpu.SemaphoreType.DMA
    vmem = pl.BlockSpec(memory_space=pltpu.VMEM)
    hbm = pl.BlockSpec(memory_space=pl.ANY)
    cleaned_real, cleaned_imag, estimate = pl.pallas_call(
        kernel,
        out_shape=(
            pltpu.VMEM((SEGS, bins), F32),
            pltpu.VMEM((SEGS, bins), F32),
            pltpu.VMEM((1, LANES), F32),
        ),
        in_specs=[hbm] * 6,
        out_specs=(vmem, vmem, vmem),
        scratch_shapes=[
            pltpu.VMEM(magnet_real.shape, magnet_real.dtype),
            pltpu.VMEM(magnet_imag.shape, magnet_imag.dtype),
            pltpu.VMEM(detector_real.shape, detector_real.dtype),
            pltpu.VMEM(detector_imag.shape, detector_imag.dtype),
            pltpu.SMEM((SEGS,), jnp.int32),
            pltpu.VMEM((TILES, LANES), F32),
            pltpu.VMEM((32, ROWS, LANES), F32),
            pltpu.VMEM((32, ROWS, LANES), F32),
            pltpu.VMEM((32, ROWS, LANES), F32),
            pltpu.VMEM((28, ROWS, LANES), F32),
            pltpu.VMEM((8, ROWS, LANES), F32),
            pltpu.VMEM((TILES, WROWS, LANES), F32),
            pltpu.VMEM((TILES, 32, LANES), F32),
            pltpu.VMEM((8, LANES), F32),
            pltpu.VMEM((NY, 16, LANES), F32),
            dma((12,)), dma((4,)), dma((5,)), dma((8,)), dma((26,)), dma((8,)), dma((7,)),
            dma((2, 8)), dma((8,)), dma((8,)), dma((3,)),
        ],
        compiler_params=pltpu.CompilerParams(collective_id=0, has_side_effects=True),
    )(
        magnet_real, magnet_imag, detector_real, detector_imag,
        valid, intersection.reshape(TILES, LANES),
    )
    return cleaned_real, cleaned_imag, estimate[0, :SEGS]


def solution(mesh):
    assert mesh.shape["seg"] == NZ * NX * 2 and mesh.shape["bin"] == NY
    torus = Mesh(mesh.devices.reshape(NZ, NX, 2, NY), ("seg_0", "seg_1", "seg_2", "bin"))
    spec3 = P(SEG, None, "bin")
    return jax.shard_map(
        on_device, mesh=torus,
        in_specs=(spec3, spec3, spec3, spec3, P(SEG), P("bin")),
        out_specs=(P(SEG, "bin"), P(SEG, "bin"), P(SEG)),
        check_vma=False,
    )
```

time: 57.4 us -> 48.9 us (0.85)
  Pallas kernels: 51.9 us -> 46.2 us
  local copies, waits for them, and re-layouts: 4.17 us -> 1.92 us
    pallas_call x1, Pallas kernels: 51.9 us -> 46.2 us  [on_device(): pl.pallas_call(kernel, out_shape=(pltpu.VMEM((SEGS, bins), F32), pltpu.VM...]
    unnamed x8 -> x2, local copies, waits for them, and re-layouts: 3.65 us -> 1.41 us
where the time goes in v2:
time: 48.9 us; the launch traced here: 48.8 us
  Pallas kernels  46.2 us (94%)
  local copies, waits for them, and re-layouts  1.92 us (4%)
  between operations  0.64 us (1%)
    pallas_call x1, Pallas kernels, on_device(): pl.pallas_call(kernel, out_shape=(pltpu.VMEM((SEGS, bins), F32), pltpu.VM...  46.2 us
    unnamed x2, local copies, waits for them, and re-layouts  1.41 us

profile of v2, /device:TPU:1, one launch (start us, length us, event | category | flops | bytes accessed | tf_op | source)
XLA Modules:
  0.0 48.8 jit_solution(15593351363297676352)
XLA Ops:
  0.6 46.2 %shard_map.85 = (f32[8,8192]{1,0:T(8,128)S(1)}, f32[8,8192]{1,0:T(8,128)S(1)}, f32[1,128]{1,0:T(1,128)S(1)}) custom-call(bf16[8,8,8192]{2,1,0:T(8,128)(2,1)} %mr_hbm.1, bf16[8,8,8192]{2,1,0:T(8,128)(2,1)} %mi_hbm.1, bf16[8,2,8192]{2,1,0:T(2,128)(2,1)} %dr_hbm.1, bf16[8,2,8192]{2,1,0:T(2,128)(2,1)} %di_hbm.1, s32[8]{0:T(128)} %keep_hbm.1, f32[64,128]{1,0:T(8,128)} %bitcast.3), custom_call_target="tpu_custom_call" | custom-call | tf_op jit(solution)/shard_map/pallas_call | solution.py:548
  46.9 0.7 %copy.11 = f32[8,8192]{1,0:T(8,128)} copy(f32[8,8192]{1,0:T(8,128)S(1)} %get-tuple-element.9) | data formatting | bytes 524288
  47.6 0.5 %slice_bitcast_fusion = f32[8]{0:T(128)} fusion(f32[1,128]{1,0:T(1,128)S(1)} %get-tuple-element.8), kind=kLoop, calls=%fused_computation | loop fusion | bytes 64 | tf_op jit(solution)/shard_map/squeeze | solution.py:581
  48.1 0.7 %copy.12 = f32[8,8192]{1,0:T(8,128)} copy(f32[8,8192]{1,0:T(8,128)S(1)} %get-tuple-element.10) | data formatting | bytes 524288

commit v3 on v2

--- a/solution.py
+++ b/solution.py
@@ -146,7 +146,7 @@
 def kernel(
     mr_hbm, mi_hbm, dr_hbm, di_hbm, keep_hbm, inter_hbm, out_r, out_i, est,
     mr, mi, dr, di, keep, inter, acc, outbox, inbox, rbuf, pbuf, wbuf, hbuf, num, ybuf,
-    m_in, d_in, sent, p_recv, r_recv, q_recv, z_recv, x_recv, f_recv, w_recv, y_recv,
+    m_in, d_in, sent, p_recv, r_recv, q_recv, z_recv, x_recv, w_recv, y_recv,
 ):
     z, x, c = lax.axis_index("seg_0"), lax.axis_index("seg_1"), lax.axis_index("seg_2")
     y = lax.axis_index("bin")
@@ -351,27 +351,43 @@
                 far_take()
                 one_take((2, 3))
 
-    for g in range(8):
-        xo, half = ORDER0[g]
+    def load_group(g):
         with jax.named_scope(f"load{g}"):
-            if g == 0:
-                for load in small[:3]:
-                    load.wait()
             loads1[ORDER1[g]].wait()
-            if (xo, half) in ((2, 0), (1, 1), (3, 0), (0, 0)):
-                loads0[xo].wait()
-        if g == 0:
-            for load in late + small[3:]:
-                load.start()
+            if ORDER0[g] in ((2, 0), (1, 1), (3, 0), (0, 0)):
+                loads0[ORDER0[g][0]].wait()
+
+    def make_other(g):
         with jax.named_scope(f"mk_other{g}"):
             make_group(g, jnp.logical_not(on_core0), outbox)
-        if g == 0:
-            with jax.named_scope("barrier"):
-                pl.semaphore_wait(barrier, len(peers))
+
+    def make_own(g):
         with jax.named_scope(f"mk_own{g}"):
-            to_partner[g].start()
             make_group(g, on_core0, acc)
-        if g:
+
+    for load in small[:3]:
+        load.wait()
+    load_group(0)
+    for load in late + small[3:]:
+        load.start()
+    make_other(0)
+    load_group(1)
+    make_other(1)
+    with jax.named_scope("barrier"):
+        pl.semaphore_wait(barrier, len(peers))
+    to_partner[0].start()
+    to_partner[1].start()
+    make_own(0)
+    make_own(1)
+    for g in range(2, 8):
+        load_group(g)
+        make_other(g)
+        to_partner[g].start()
+        if g == 2:
+            after(0)
+            after(1)
+        make_own(g)
+        if g > 2:
             after(g - 1)
     after(7)
 
@@ -423,13 +439,21 @@
     for q in range(4):
         wbuf[mine, 8 * q : 8 * q + 8, :] = filters[q]
 
-    def w_copy(tile, recv, where):
-        return copy(wbuf.at[tile], wbuf.at[tile], sent.at[3], recv, where)
+    def w_copy(tile, recv, where, count=1):
+        block = wbuf.at[pl.ds(tile, count)]
+        return copy(block, block, sent.at[3], recv, where)
 
     far_first = (4, 3, 5, 2, 6, 1, 7)
-    along_z = {d: w_copy(mine, z_recv.at[d - 1], at_z(d)) for d in far_first}
-    for d in far_first:
-        along_z[d].start()
+
+    @pl.when(on_core0)
+    def _():
+        for d in far_first:
+            w_copy(mine, z_recv.at[d - 1], at_z(d)).start()
+
+    @pl.when(jnp.logical_not(on_core0))
+    def _():
+        for d in (2, 1, 3):
+            w_copy(mine, x_recv.at[d - 1, 0], at_x(d)).start()
 
     small[3].wait()
     square = inter[0:8, :] * inter[0:8, :]
@@ -440,11 +464,22 @@
     def tile_from(core, dz, dx):
         return tile_of(core, lax.rem(z + NZ - dz, NZ), lax.rem(x + NX - dx, NX))
 
-    def got(tile, sem, where):
-        w_copy(tile, sem, where).wait_recv()
+    def row_from(dz):
+        return 32 + 4 * lax.rem(z + NZ - dz, NZ)
+
+    def got(name, tile, sem, where, count=1):
+        with jax.named_scope(name):
+            w_copy(tile, sem, where, count).wait_recv()
 
     def cleaned(tile):
         num[...] += clean_tile(tile, mr, mi, inter, wbuf, hbuf, out_r, out_i)
+
+    def cleaned_row(dz):
+        def body(i, carry):
+            cleaned(row_from(dz) + i)
+            return carry
+
+        lax.fori_loop(0, 4, body, 0)
 
     near_first = (0, 1, 7, 2, 6, 3, 5, 4)
 
@@ -456,50 +491,79 @@
     def share(d, dx, tile):
         w_copy(tile, w_recv.at[block_of[d, dx]], partner).start()
 
-    def got_block(i):
-        with jax.named_scope(f"gp{i}"):
-            whole = wbuf.at[pl.ds(0, len(blocks[i]))]
-            copy(whole, whole, sent.at[3], w_recv.at[i], partner).wait_recv()
-
-    def clean_block(i, first=0, last=8):
-        for d, dx in blocks[i][first:last]:
-            cleaned(tile_from(1 - c, d, dx))
-
-    for d in near_first:
-        tile = tile_from(c, d, 0)
-        if d:
-            with jax.named_scope(f"gz{d}"):
-                got(tile, z_recv.at[d - 1], at_z(NZ - d))
-        for way, dx in ((0, 1), (1, 3)):
-            w_copy(tile, x_recv.at[way, d], at_x(dx)).start()
-        share(d, 0, tile)
-        cleaned(tile)
-    for i, d in enumerate(near_first):
-        for way, dx in ((0, 1), (1, 3)):
-            tile = tile_from(c, d, dx)
-            with jax.named_scope(f"gx{d}_{dx}"):
-                got(tile, x_recv.at[way, d], at_x(NX - dx))
-            if way == i % 2:
-                w_copy(tile, f_recv.at[d], at_x(dx)).start()
-            share(d, dx, tile)
+    def take_block(i):
+        got(f"gp{i}", 0, w_recv.at[i], partner, len(blocks[i]))
+        for d, dx in blocks[i]:
+            cleaned(tile_from(0, d, dx))
+
+    def share_row(dz):
+        w_copy(row_from(dz), w_recv.at[dz], partner, 4).start()
+
+    def take_row(dz):
+        got(f"gr{dz}", row_from(dz), w_recv.at[dz], partner, 4)
+        cleaned_row(dz)
+
+    @pl.when(on_core0)
+    def _():
+        for d in near_first:
+            tile = tile_from(0, d, 0)
+            if d:
+                got(f"gz{d}", tile, z_recv.at[d - 1], at_z(NZ - d))
+            for dx in (2, 1, 3):
+                w_copy(tile, x_recv.at[dx - 1, d], at_x(dx)).start()
+            share(d, 0, tile)
             cleaned(tile)
-    for i, d in enumerate(near_first):
-        if i in (0, 1):
-            got_block(i)
-            clean_block(i)
-        if i in (2, 4):
-            got_block(i // 2 + 1)
-            clean_block(i // 2 + 1, 0, 4)
-        if i in (3, 5):
-            clean_block(i // 2 + 1, 4, 8)
-        tile = tile_from(c, d, 2)
-        with jax.named_scope(f"gf{d}"):
-            got(tile, f_recv.at[d], at_x(1 if i % 2 == 1 else 3))
-        share(d, 2, tile)
-        cleaned(tile)
-    for i in range(4, 8):
-        got_block(i)
-        clean_block(i)
+        take_row(0)
+        for i, d in enumerate(near_first):
+            for dx in (1, 3):
+                tile = tile_from(0, d, dx)
+                got(f"gx{d}_{dx}", tile, x_recv.at[dx - 1, d], at_x(NX - dx))
+                share(d, dx, tile)
+                cleaned(tile)
+        for i, d in enumerate(near_first):
+            tile = tile_from(0, d, 2)
+            got(f"gf{d}", tile, x_recv.at[1, d], at_x(2))
+            share(d, 2, tile)
+            cleaned(tile)
+            if i in (1, 3, 5, 7):
+                take_row((1, 7, 2, 6)[i // 2])
+        for d in (3, 5, 4):
+            take_row(d)
+
+    @pl.when(jnp.logical_not(on_core0))
+    def _():
+        cleaned(mine)
+        for dx in (1, 3, 2):
+            got(f"rx{dx}", tile_from(1, 0, dx), x_recv.at[dx - 1, 0], at_x(NX - dx))
+        for d in (2, 6, 1, 7):
+            w_copy(row_from(0), z_recv.at[d - 1], at_z(d), 4).start()
+        share_row(0)
+        for dx in (1, 3, 2):
+            cleaned(tile_from(1, 0, dx))
+        for d, onward, half in ((2, 1, 0), (6, 7, 2)):
+            got(f"rz{d}", row_from(d), z_recv.at[d - 1], at_z(NZ - d), 4)
+            w_copy(row_from(d) + half, z_recv.at[3 if half == 0 else 7], at_z(d), 2).start()
+            w_copy(row_from(d), z_recv.at[2 if half == 0 else 4], at_z(onward), 4).start()
+            share_row(d)
+        for d in (1, 7):
+            got(f"rz{d}", row_from(d), z_recv.at[d - 1], at_z(NZ - d), 4)
+            share_row(d)
+        take_block(0)
+        for d in (1, 7, 2, 6):
+            cleaned_row(d)
+        take_block(1)
+        take_block(2)
+        take_block(3)
+        for d, back in ((3, 7), (5, 1)):
+            got(f"rz{d}", row_from(d), z_recv.at[d - 1], at_z(back), 4)
+            share_row(d)
+            cleaned_row(d)
+        got("rz4a", row_from(4), z_recv.at[3], at_z(6), 2)
+        got("rz4b", row_from(4) + 2, z_recv.at[7], at_z(2), 2)
+        share_row(4)
+        cleaned_row(4)
+        for i in range(4, 8):
+            take_block(i)
 
     with jax.named_scope("ysum"):
         ybuf[y, 0:8, :] = num[...]
@@ -570,8 +634,8 @@
             pltpu.VMEM((TILES, 32, LANES), F32),
             pltpu.VMEM((8, LANES), F32),
             pltpu.VMEM((NY, 16, LANES), F32),
-            dma((12,)), dma((4,)), dma((5,)), dma((8,)), dma((26,)), dma((8,)), dma((7,)),
-            dma((2, 8)), dma((8,)), dma((8,)), dma((3,)),
+            dma((12,)), dma((4,)), dma((5,)), dma((8,)), dma((26,)), dma((8,)), dma((8,)),
+            dma((3, 8)), dma((8,)), dma((3,)),
         ],
         compiler_params=pltpu.CompilerParams(collective_id=0, has_side_effects=True),
     )(

time: 48.9 us -> 47.6 us (0.973)
  Pallas kernels: 46.2 us -> 44.8 us
    pallas_call x1, Pallas kernels: 46.2 us -> 44.8 us  [on_device(): pl.pallas_call(kernel, out_shape=(pltpu.VMEM((SEGS, bins), F32), pltpu.VM...]
where the time goes in v3:
time: 47.6 us; the launch traced here: 47.3 us
  Pallas kernels  44.8 us (94%)
  local copies, waits for them, and re-layouts  1.92 us (4%)
  between operations  0.64 us (1%)
    pallas_call x1, Pallas kernels, on_device(): pl.pallas_call(kernel, out_shape=(pltpu.VMEM((SEGS, bins), F32), pltpu.VM...  44.8 us
    unnamed x2, local copies, waits for them, and re-layouts  1.41 us

profile of v3, /device:TPU:1, one launch (start us, length us, event | category | flops | bytes accessed | tf_op | source)
XLA Modules:
  0.0 47.3 jit_solution(6660434831081748557)
XLA Ops:
  0.6 44.8 %shard_map.85 = (f32[8,8192]{1,0:T(8,128)S(1)}, f32[8,8192]{1,0:T(8,128)S(1)}, f32[1,128]{1,0:T(1,128)S(1)}) custom-call(bf16[8,8,8192]{2,1,0:T(8,128)(2,1)} %mr_hbm.1, bf16[8,8,8192]{2,1,0:T(8,128)(2,1)} %mi_hbm.1, bf16[8,2,8192]{2,1,0:T(2,128)(2,1)} %dr_hbm.1, bf16[8,2,8192]{2,1,0:T(2,128)(2,1)} %di_hbm.1, s32[8]{0:T(128)} %keep_hbm.1, f32[64,128]{1,0:T(8,128)} %bitcast.3), custom_call_target="tpu_custom_call" | custom-call | tf_op jit(solution)/shard_map/pallas_call | solution.py:612
  45.4 0.7 %copy.11 = f32[8,8192]{1,0:T(8,128)} copy(f32[8,8192]{1,0:T(8,128)S(1)} %get-tuple-element.9) | data formatting | bytes 524288
  46.1 0.5 %slice_bitcast_fusion = f32[8]{0:T(128)} fusion(f32[1,128]{1,0:T(1,128)S(1)} %get-tuple-element.8), kind=kLoop, calls=%fused_computation | loop fusion | bytes 64 | tf_op jit(solution)/shard_map/squeeze | solution.py:645
  46.6 0.7 %copy.12 = f32[8,8192]{1,0:T(8,128)} copy(f32[8,8192]{1,0:T(8,128)S(1)} %get-tuple-element.10) | data formatting | bytes 524288
